TPU v7x, 32 devices: a whole 2x2x4 slice. The times are simulated.
32 devices in a mesh: seq: 8 (over z, y), tp: 4 (over x, core).
Axes of the slice: x: 2, y: 2, z: 4, core: 2. Of those that a mesh axis runs over, the one named last changes fastest.
Arguments:
- tokens: bfloat16 [4096, 2560], P('seq', 'tp'), may hold values from -6 to 6
- gate_weight: bfloat16 [2560, 5120], P(None, 'tp'), may hold values from -0.125 to 0.125
- inner_weight: bfloat16 [2560, 5120], P(None, 'tp'), may hold values from -0.125 to 0.125
- state_weight: bfloat16 [2560, 256], replicated, may hold values from -0.125 to 0.125
- step_weight: bfloat16 [2560, 80], P(None, 'tp'), may hold values from -0.125 to 0.125
- conv_inner: float32 [4, 5120], P(None, 'tp'), may hold values from -3 to 3
- conv_state: float32 [4, 256], replicated, may hold values from -3 to 3
- step_bias: float32 [80], P('tp'), may hold values from -3 to 1
- decay_rate: float32 [80], P('tp'), may hold values from 1e-05 to 0.02
- skip_gain: float32 [80], P('tp'), may hold values from 0.5 to 2
- norm_gain: float32 [5120], P('tp'), may hold values from 0.1 to 1.9
- out_weight: bfloat16 [5120, 2560], P('tp'), may hold values from -0.078125 to 0.078125
Outputs:
- layer_out: bfloat16 [4096, 2560], P(('seq', 'tp'))
All inputs are finite; a program needn't handle non-finite values.
Results may differ from a plain program's by a relative error of at most 0.018.
Values may be sent and summed in bfloat16 or wider, within the bound.
A program may use at most 128 MiB of HBM per device.

v0:
```python
import jax
import jax.numpy as jnp
from jax import lax
from jax.sharding import PartitionSpec as P

GROUP = 256
HIGHEST = lax.Precision.HIGHEST


def passed_along(shard, axis, by):
    size = lax.axis_size(axis)
    pairs = [(i, i + by) for i in range(size) if 0 <= i + by < size]
    return lax.ppermute(shard, axis, pairs)


def group_decay(inner_blk, inject_blk, step_blk, log_blk):
    cumulative = jnp.cumsum(log_blk, axis=0)
    ending = cumulative[-1]
    tail_weight = jnp.exp(ending[None, :] - cumulative) * step_blk
    scaled = inner_blk.astype(jnp.float32) * tail_weight[:, :, None]
    contribution = jnp.einsum(
        "thp,tn->hpn", scaled, inject_blk.astype(jnp.float32), precision=HIGHEST
    )
    return (cumulative, ending, contribution)


def group_intra(inner_blk, inject_blk, readout_blk, step_blk, cumulative):
    scores = jnp.dot(readout_blk, inject_blk.T, preferred_element_type=jnp.float32)
    length = scores.shape[0]
    causal = jnp.arange(length)[:, None] >= jnp.arange(length)[None, :]
    log_gaps = cumulative.T[:, :, None] - cumulative.T[:, None, :]
    decay_mask = jnp.exp(jnp.where(causal[None], log_gaps, -jnp.inf))
    mixing = (scores[None] * decay_mask * step_blk.T[:, None, :]).astype(jnp.bfloat16)
    return jnp.einsum("hts,shp->thp", mixing, inner_blk, preferred_element_type=jnp.float32)


def read_state(readout_blk, cumulative, carried):
    reads = jnp.einsum("tn,hpn->thp", readout_blk.astype(jnp.float32), carried, precision=HIGHEST)
    return reads * jnp.exp(cumulative)[:, :, None]


def fold_states(own_index, prefix, decay_all):
    own_prefix = lax.dynamic_index_in_dim(prefix, own_index, 0, keepdims=False)

    def absorb(carried, segment, first_row):
        row_count = segment.shape[0]
        positions = jnp.arange(row_count, dtype=jnp.int32)
        exponent = own_prefix[None, :] - prefix - decay_all
        factor = jnp.exp(jnp.where((positions < own_index)[:, None], exponent, -jnp.inf))
        return carried + jnp.einsum("kh,khpn->hpn", factor, segment, precision=HIGHEST)

    return absorb


def receive(decay_total, local_state):
    zero_state = jnp.zeros_like(local_state)
    decay_all = lax.all_gather(decay_total[None, :], "seq", axis=0, tiled=True)
    prefix = jnp.cumsum(decay_all, axis=0) - decay_all
    absorb = fold_states(lax.axis_index("seq"), prefix, decay_all)
    return absorb(
        zero_state,
        lax.all_gather(local_state[None].astype(jnp.bfloat16), "seq", axis=0, tiled=True).astype(
            jnp.float32
        ),
        jnp.int32(0),
    )


def on_device(
    tokens,
    gate_weight,
    inner_weight,
    state_weight,
    step_weight,
    conv_inner,
    conv_state,
    step_bias,
    decay_rate,
    skip_gain,
    norm_gain,
    out_weight,
):
    tok_rows = tokens.shape[0]
    weights = (gate_weight, inner_weight, state_weight, step_weight)
    segment = lax.all_gather(tokens, "tp", axis=1, tiled=True)
    gate_raw, inner_raw, state_raw, step_raw = tuple(
        (jnp.dot(segment, weight, preferred_element_type=jnp.float32) for weight in weights)
    )
    gate_act = gate_raw.astype(jnp.bfloat16)
    mixed_in = jnp.concatenate([inner_raw, state_raw], axis=1).astype(jnp.bfloat16)
    taps = conv_inner.shape[0]
    edge_rows = passed_along(mixed_in[tok_rows - (taps - 1) :], "seq", 1)
    padded = jnp.concatenate([edge_rows, mixed_in], axis=0)
    kernel = jnp.concatenate([conv_inner, conv_state], axis=1)
    conv_sum = jnp.zeros(mixed_in.shape, jnp.float32)
    for tap in range(taps):
        conv_sum = (
            conv_sum + padded[tap : tap + tok_rows].astype(jnp.float32) * kernel[tap][None, :]
        )
    conv_out = jax.nn.silu(conv_sum).astype(jnp.bfloat16)
    width_inner = inner_weight.shape[1]
    head_count = step_weight.shape[1]
    head_width = width_inner // head_count
    state_size = state_weight.shape[1] // 2
    inner_act = conv_out[:, :width_inner].reshape(tok_rows, head_count, head_width)
    inject = conv_out[:, width_inner : width_inner + state_size]
    readout = conv_out[:, width_inner + state_size :]
    time_step = jax.nn.softplus(step_raw + step_bias[None, :])
    log_decay = -time_step * decay_rate[None, :]
    block_count = tok_rows // GROUP
    pieces = []
    for group_number in range(block_count):
        row_span = slice(group_number * GROUP, (group_number + 1) * GROUP)
        pieces.append(
            (
                inner_act[row_span],
                inject[row_span],
                readout[row_span],
                time_step[row_span],
                log_decay[row_span],
            )
        )
    outputs = []
    local_state = jnp.zeros((head_count, head_width, state_size), jnp.float32)
    decay_total = jnp.zeros((head_count,), jnp.float32)
    summaries = []
    for group_number in range(block_count):
        inner_blk, inject_blk, readout_blk, step_blk, log_blk = pieces[group_number]
        cumulative, ending, contribution = group_decay(inner_blk, inject_blk, step_blk, log_blk)
        local_state = jnp.exp(ending)[:, None, None] * local_state + contribution
        decay_total = decay_total + ending
        summaries.append((cumulative, ending, contribution))
    carried = receive(decay_total, local_state)
    for group_number in range(block_count):
        inner_blk, inject_blk, readout_blk, step_blk, log_blk = pieces[group_number]
        cumulative, ending, contribution = summaries[group_number]
        block_out = group_intra(inner_blk, inject_blk, readout_blk, step_blk, cumulative)
        outputs.append(block_out + read_state(readout_blk, cumulative, carried))
        carried = jnp.exp(ending)[:, None, None] * carried + contribution
    ssd_out = jnp.concatenate(outputs, axis=0) + skip_gain[None, :, None] * inner_act.astype(
        jnp.float32
    )
    gated = ssd_out.reshape(tok_rows, width_inner) * jax.nn.silu(gate_act.astype(jnp.float32))
    square_total = lax.psum(jnp.sum(gated * gated, axis=1), "tp")
    mean_square = square_total / (width_inner * lax.axis_size("tp"))
    normed = (gated * lax.rsqrt(mean_square + 1e-05)[:, None] * norm_gain[None, :]).astype(
        jnp.bfloat16
    )
    return lax.psum_scatter(
        jnp.dot(normed, out_weight, preferred_element_type=jnp.float32).astype(jnp.bfloat16),
        "tp",
        scatter_dimension=0,
        tiled=True,
    )


def solution(mesh):
    in_specs = (
        P("seq", "tp"),
        P(None, "tp"),
        P(None, "tp"),
        P(),
        P(None, "tp"),
        P(None, "tp"),
        P(),
        P("tp"),
        P("tp"),
        P("tp"),
        P("tp"),
        P("tp", None),
    )
    out_specs = P(("seq", "tp"), None)
    return jax.shard_map(
        on_device, mesh=mesh, in_specs=in_specs, out_specs=out_specs, check_vma=False
    )
```

profile of v0, /device:TPU:0, one launch (start us, length us, event | category | flops | bytes accessed | tf_op | source)
XLA Modules:
  0.0 202.1 jit_solution(8216762679849479591)
XLA Ops:
  6.5 0.7 all-gather.5.cloned.1.call-update
  7.3 0.7 constant_dynamic-update-slice_fusion.1
  8.0 0.7 constant_dynamic-update-slice_fusion
  8.8 28.4 %all-gather.5.cloned.1.call-done = bf16[512,2560]{1,0:T(8,128)(2,1)} async-done(((bf16[512,640]{1,0:T(8,128)(2,1)}), bf16[512,2560]{1,0:T(8,128)(2,1)}) %all-gather.5.cloned.1.call-update) | async-done | bytes 2621456 | tf_op jit(solution)/shard_map/all_gather | solution.py:85
  37.2 2.6 %negate_multiply_fusion = (f32[512,20]{0,1:T(8,128)S(1)}, f32[512,20]{0,1:T(8,128)S(1)}) fusion(f32[20]{0:T(128)} %param.20, f32[20]{0:T(128)} %param.19, bf16[512,2560]{1,0:T(8,128)(2,1)} %all-gather.5.cloned.1.call-done, bf16[2560,20]{0,1:T(8,128)(2,1)} %param.16), kind=kOutput, calls=%fused_computation.74 | convolution fusion | flops 52520960 | bytes 2805920 | tf_op jit(solution)/shard_map/dot_general | solution.py:87
  41.8 7.3 %convolution_convert_fusion.2 = bf16[512,1280]{1,0:T(8,128)(2,1)S(1)} fusion(bf16[512,2560]{1,0:T(8,128)(2,1)} %all-gather.5.cloned.1.call-done, bf16[2560,1280]{1,0:T(8,128)(2,1)} %param.14), kind=kOutput, calls=%fused_computation.7 | convolution fusion | flops 3356098560 | bytes 10485760 | tf_op jit(solution)/shard_map/dot_general | solution.py:87
  49.2 0.8 convolution_convert_fusion.3
  50.0 3.4 %collective-permute-start = (bf16[3,1536]{1,0:T(4,128)(2,1)S(1)}, bf16[3,1536]{1,0:T(4,128)(2,1)S(1)}, u32[]{:S(2)}, u32[]{:S(2)}) collective-permute-start(bf16[3,1536]{1,0:T(4,128)(2,1)S(1)} %fusion.57), channel_id=1, source_target_pairs={{0,4},{4,8},{8,12},{12,16},{16,20},{20,24},{24,28},{1,5},{5,9},{9,... | collective-permute-start | bytes 27656 | tf_op jit(solution)/shard_map/ppermute | solution.py:13
  53.6 0.7 slice_bitcast_fusion.3
  55.3 2.0 multiply_convert_fusion.2
  57.2 0.9 fusion.60
  58.2 2.2 %copy.34 = bf16[256,1280]{0,1:T(8,128)(2,1)} copy(bf16[256,1280]{1,0:T(8,128)(2,1)} %get-tuple-element.12) | data formatting | bytes 1310720 | tf_op jit(solution)/shard_map/slice | solution.py:116
  60.3 1.1 copy.39
  61.4 1.9 fusion.29
  63.3 2.6 %fusion.35 = bf16[20,64,128]{2,1,0:T(8,128)(2,1)} fusion(bf16[256,20,64]{0,2,1:T(8,128)(2,1)} %bitcast.69, f32[256,20]{0,1:T(8,128)} %get-tuple-element.17, f32[20,64,128]{2,1,0:T(8,128)S(1)} %fusion.29, f32[20]{0:T(128)S(1)} %get-tuple-element.23, f32[20]{0:T(128)S(1)} %exp.52, bf16[512,1536]{1,0:T(8,128)(2,1)S(1)} %multiply_convert_fusion.2), kind=kOutput, calls=%fused_computation.50 | convolution fusion | flops 504627200 | bytes 1725440 | tf_op jit(solution)/shard_map/thp,tn->hpn/dot_general | solution.py:21
  66.0 0.7 mul.225
  66.7 0.7 mul.226
  67.4 0.6 iota_compare_fusion
  68.0 21.5 %all-gather.1 = f32[8,1,20]{2,1,0:T(1,128)S(1)} all-gather(f32[1,1,20]{2,1,0:T(1,128)S(1)} %bitcast.84), channel_id=1, replica_groups=mesh['seq'=8,'tp'=4] {'seq'}, dimensions={0}, use_global_device_ids=true | all-gather | bytes 720 | tf_op jit(solution)/shard_map/all_gather | solution.py:57
  90.2 3.9 %fusion.21 = f32[256,20,64]{0,2,1:T(8,128)} fusion(bf16[256,20,64]{0,2,1:T(8,128)(2,1)} %bitcast.72, f32[20,256]{1,0:T(8,128)} %get-tuple-element.14, f32[20,256]{1,0:T(8,128)} %bitcast.75, f32[256,256]{1,0:T(8,128)S(1)} %fusion.53, pred[256,256]{1,0:T(8,128)(4,1)} %iota_compare_fusion), kind=kOutput, calls=%fused_computation.36 | convolution fusion | flops 174325760 | bytes 2334720 | tf_op jit(solution)/shard_map/hts,shp->thp/dot_general | solution.py:34
  94.1 2.7 %fusion.20 = f32[256,20,64]{0,2,1:T(8,128)} fusion(bf16[256,20,64]{0,2,1:T(8,128)(2,1)S(1)} %bitcast.70, f32[20,256]{1,0:T(8,128)S(1)} %copy-done.10, f32[20,256]{1,0:T(8,128)S(1)} %bitcast.78, f32[256,256]{1,0:T(8,128)S(1)} %fusion.48, pred[256,256]{1,0:T(8,128)(4,1)S(1)} %copy-done.9), kind=kOutput, calls=%fused_computation.35 | convolution fusion | flops 174325760 | bytes 2334720 | tf_op jit(solution)/shard_map/hts,shp->thp/dot_general | solution.py:34
  96.9 24.3 %all-gather.7.cloned.1.call-done = bf16[160,64,128]{2,1,0:T(8,128)(2,1)} async-done(((bf16[20,64,128]{2,1,0:T(8,128)(2,1)}), bf16[160,64,128]{2,1,0:T(8,128)(2,1)}) %all-gather.7.cloned.1.call-update) | async-done | bytes 2621456 | tf_op jit(solution)/shard_map/all_gather | solution.py:62
  121.2 5.0 %fusion.6 = f32[20,1,64,128]{3,1,2,0:T(1,128)S(1)} fusion(f32[8,20,1,1]{0,2,3,1:T(1,128)S(1)} %copy.43, bf16[8,20,64,128]{3,2,1,0:T(8,128)(2,1)} %bitcast.68), kind=kOutput, calls=%fused_computation.15 | convolution fusion | flops 15728640 | bytes 3277440 | tf_op jit(solution)/shard_map/kh,khpn->hpn/dot_general | solution.py:50
  126.2 0.8 copy-done.1
  127.0 1.8 fusion.22
  128.8 2.8 %copy.40 = f32[256,1280]{1,0:T(8,128)} copy(f32[256,1280]{0,1:T(8,128)} %bitcast.66) | data formatting | bytes 2621440 | tf_op jit(solution)/shard_map/concatenate | solution.py:140
  131.6 3.3 %fusion.23 = f32[256,20,64]{0,2,1:T(8,128)} fusion(f32[256,20,64]{0,2,1:T(8,128)} %fusion.20, f32[256,20]{0,1:T(8,128)} %get-tuple-element.20, f32[20,64,128]{2,1,0:T(8,128)S(1)} %fusion.29, f32[20,64,128]{2,1,0:T(8,128)} %bitcast.65, f32[20]{0:T(128)S(1)} %copy-done.12, bf16[512,1536]{1,0:T(8,128)(2,1)S(1)} %multiply_convert_fusion.2), kind=kOutput, calls=%fused_computation.40 | convolution fusion | flops 504299520 | bytes 4018688 | tf_op jit(solution)/shard_map/tn,hpn->thp/dot_general | solution.py:38
  134.9 2.9 %copy.41 = f32[256,1280]{1,0:T(8,128)} copy(f32[256,1280]{0,1:T(8,128)} %bitcast.67) | data formatting | bytes 2621440 | tf_op jit(solution)/shard_map/concatenate | solution.py:140
  137.8 9.8 %multiply_reduce_fusion = (f32[512]{0:T(512)S(1)}, f32[512,1280]{1,0:T(8,128)}) fusion(bf16[512,2560]{1,0:T(8,128)(2,1)} %all-gather.5.cloned.1.call-done, bf16[2560,1280]{1,0:T(8,128)(2,1)} %param.13, bf16[512,1536]{1,0:T(8,128)(2,1)S(1)} %multiply_convert_fusion.2, f32[1280]{0:T(1024)S(1)} %copy-done.11, f32[256,1280]{1,0:T(8,128)} %copy.41, ...), kind=kOutput, calls=%fused_computation.18 | convolution fusion | flops 3363962368 | bytes 15735808 | tf_op jit(solution)/shard_map/dot_general | solution.py:87
  147.6 5.6 %psum.7 = f32[512]{0:T(512)S(1)} all-reduce(f32[512]{0:T(512)S(1)} %get-tuple-element.26), channel_id=1, replica_groups=mesh['seq'=8,'tp'=4] {'tp'}, use_global_device_ids=true, to_apply=%region_6.7 | all-reduce | flops 512 | bytes 4096 | tf_op jit(solution)/shard_map/psum | solution.py:144
  153.3 8.8 %convolution_convert_fusion = bf16[512,2560]{1,0:T(8,128)(2,1)} fusion(bf16[1280,2560]{1,0:T(8,128)(2,1)} %param.23, f32[512,1280]{1,0:T(8,128)} %get-tuple-element.27, f32[1280]{0:T(1024)S(1)} %copy-done.13, f32[512]{0:T(512)S(1)} %add_rsqrt_fusion), kind=kOutput, calls=%fused_computation.2 | convolution fusion | flops 3358720000 | bytes 11803648 | tf_op jit(solution)/shard_map/dot_general | solution.py:150
  162.1 33.5 %reduce-scatter.2.cloned.1.call-done = bf16[128,2560]{1,0:T(8,128)(2,1)} async-done(((bf16[512,2560]{1,0:T(8,128)(2,1)}), bf16[128,2560]{1,0:T(8,128)(2,1)}) %reduce-scatter.2.cloned.1.call-update) | async-done | bytes 655376 | tf_op jit(solution)/shard_map/reduce_scatter | solution.py:149
  (69 shorter events, 3.8 us)
Async XLA Ops:
  6.5 42.6 %copy-start = (bf16[2560,256]{1,0:T(8,128)(2,1)S(1)}, bf16[2560,256]{1,0:T(8,128)(2,1)}, u32[]{:S(2)}) copy-start(bf16[2560,256]{1,0:T(8,128)(2,1)} %param.15) | copy-start | bytes 3932164
  6.5 30.6 %all-gather.5.cloned.1.call-start = ((), (), s32[]{:S(2)}) async-start(), calls=%async_computation.1 | async-start | bytes 3276800 | tf_op jit(solution)/shard_map/all_gather | solution.py:85
  7.3 113.9 %all-gather.7.cloned.1.call-start = ((), (), s32[]{:S(2)}) async-start(), calls=%async_computation.3 | async-start | bytes 2949120 | tf_op jit(solution)/shard_map/all_gather | solution.py:62
  40.8 12.8 %copy-start.5 = (f32[3,8,2,128]{3,1,2,0:T(8,128)}, f32[3,8,2,128]{3,1,2,0:T(8,128)S(1)}, u32[]{:S(2)}) copy-start(f32[3,8,2,128]{3,1,2,0:T(8,128)S(1)} %copy.46) | copy-start | bytes 73732
  41.8 11.9 %copy-start.6 = (f32[3,8,2,128]{3,1,2,0:T(8,128)}, f32[3,8,2,128]{3,1,2,0:T(8,128)S(1)}, u32[]{:S(2)}) copy-start(f32[3,8,2,128]{3,1,2,0:T(8,128)S(1)} %copy.47) | copy-start | bytes 73732
  41.8 7.4 %copy-start.3 = (bf16[512,2560]{1,0:T(8,128)(2,1)S(1)}, bf16[512,2560]{1,0:T(8,128)(2,1)}, u32[]{:S(2)}) copy-start(bf16[512,2560]{1,0:T(8,128)(2,1)} %all-gather.5.cloned.1.call-done) | copy-start | bytes 7864324
  50.0 4.9 %collective-permute-start = (bf16[3,1536]{1,0:T(4,128)(2,1)S(1)}, bf16[3,1536]{1,0:T(4,128)(2,1)S(1)}, u32[]{:S(2)}, u32[]{:S(2)}) collective-permute-start(bf16[3,1536]{1,0:T(4,128)(2,1)S(1)} %fusion.57), channel_id=1, source_target_pairs={{0,4},{4,8},{8,12},{12,16},{16,20},{20,24},{24,28},{1,5},{5,9},{9,... | collective-permute-start | bytes 27656 | tf_op jit(solution)/shard_map/ppermute | solution.py:13
  65.9 129.7 %reduce-scatter.2.cloned.1.call-start = ((), (), s32[]{:S(2)}) async-start(), calls=%async_computation.2 | async-start | bytes 3276800 | tf_op jit(solution)/shard_map/reduce_scatter | solution.py:149
  90.1 4.0 %copy-start.2 = (bf16[256,1280]{0,1:T(8,128)(2,1)S(1)}, bf16[256,1280]{0,1:T(8,128)(2,1)}, u32[]{:S(2)}) copy-start(bf16[256,1280]{0,1:T(8,128)(2,1)} %copy.39) | copy-start | bytes 1966084
  90.1 4.0 %copy-start.7 = (f32[3,8,2,128]{3,1,2,0:T(8,128)S(1)}, f32[3,8,2,128]{3,1,2,0:T(8,128)}, u32[]{:S(2)}) copy-start(f32[3,8,2,128]{3,1,2,0:T(8,128)} %copy-done.6) | copy-start | bytes 73732
  90.1 4.0 %copy-start.9 = (pred[256,256]{1,0:T(8,128)(4,1)S(1)}, pred[256,256]{1,0:T(8,128)(4,1)}, u32[]{:S(2)}) copy-start(pred[256,256]{1,0:T(8,128)(4,1)} %iota_compare_fusion) | copy-start | bytes 196612
  90.2 4.0 %copy-start.10 = (f32[20,256]{1,0:T(8,128)S(1)}, f32[20,256]{1,0:T(8,128)}, u32[]{:S(2)}) copy-start(f32[20,256]{1,0:T(8,128)} %get-tuple-element.16) | copy-start | bytes 61444
  121.2 5.8 %copy-start.4 = (f32[256,20,64]{0,2,1:T(8,128)S(1)}, f32[256,20,64]{0,2,1:T(8,128)}, u32[]{:S(2)}) copy-start(f32[256,20,64]{0,2,1:T(8,128)} %fusion.21) | copy-start | bytes 3932164
  121.2 5.8 %copy-start.8 = (f32[256,20]{0,1:T(8,128)S(1)}, f32[256,20]{0,1:T(8,128)}, u32[]{:S(2)}) copy-start(f32[256,20]{0,1:T(8,128)} %get-tuple-element.21) | copy-start | bytes 61444
  126.2 0.8 copy-start.1
  127.0 4.6 %copy-start.12 = (f32[20]{0:T(128)S(1)}, f32[20]{0:T(128)}, u32[]{:S(2)}) copy-start(f32[20]{0:T(128)} %get-tuple-element.22) | copy-start | bytes 244
  131.6 6.2 %copy-start.11 = (f32[1280]{0:T(1024)S(1)}, f32[1280]{0:T(1024)}, u32[]{:S(2)}) copy-start(f32[1280]{0:T(1024)} %mul.226) | copy-start | bytes 15364
  137.8 15.5 %copy-start.13 = (f32[1280]{0:T(1024)S(1)}, f32[1280]{0:T(1024)}, u32[]{:S(2)}) copy-start(f32[1280]{0:T(1024)} %param.22) | copy-start | bytes 15364
Sparse Core Ops, SparseCore 0:
  8.9 28.2 all-gather.4
  66.0 55.1 all-gather.6
  162.2 33.3 reduce-scatter.1
where the time goes:
time: 203 us; the launch traced here: 202 us
  waiting for transfers between devices  86.9 us (43%)
  matrix products  51 us (25%)
  blocking collectives  27.2 us (13%)
  local copies, waits for them, and re-layouts  14.2 us (7%)
  between operations  13.4 us (7%)
  other arithmetic  5.98 us (3%)
  starting transfers between devices  3.46 us (2%)
    reduce_scatter x1, waiting for transfers between devices, on_device(): lax.psum_scatter(jnp.dot(normed, out_weight, preferred_element_type=jnp.f...  33.5 us
    all_gather x1, waiting for transfers between devices, on_device(): segment = lax.all_gather(tokens, 'tp', axis=1, tiled=True)  28.4 us
    all_gather x1, waiting for transfers between devices, receive(): lax.all_gather(local_state[None].astype(jnp.bfloat16), 'seq', axis=0, til...  24.3 us
    all_gather x1, blocking collectives, receive(): decay_all = lax.all_gather(decay_total[None, :], 'seq', axis=0, tiled=True)  21.5 us
    dot_general x4, matrix products, on_device(): jnp.dot(segment, weight, preferred_element_type=jnp.float32)  20.7 us
    dot_general x1, matrix products, on_device(): jnp.dot(normed, out_weight, preferred_element_type=jnp.float32)  8.79 us
    dot_general x2, matrix products, group_intra(): jnp.einsum('hts,shp->thp', mixing, inner_blk, preferred_element_type=jnp....  6.67 us
    concatenate x2, local copies, waits for them, and re-layouts, on_device(): jnp.concatenate(outputs, axis=0)  5.7 us
  transfers between devices with their start and end apart: 4, of which 3 were waited for; matrix products, arithmetic and copies ran while one was open for 6% of the time, Pallas kernels for 0%

commit v1 on v0

--- a/solution.py
+++ b/solution.py
@@ -82,7 +82,12 @@
 ):
     tok_rows = tokens.shape[0]
     weights = (gate_weight, inner_weight, state_weight, step_weight)
-    segment = lax.all_gather(tokens, "tp", axis=1, tiled=True)
+    ring = [tokens]
+    for hop in range(3):
+        ring.append(lax.ppermute(ring[-1], "tp", [(dev, (dev + 1) % 4) for dev in range(4)]))
+    segment = jnp.roll(
+        jnp.concatenate(ring[::-1], axis=1), (lax.axis_index("tp") + 1) * ring[0].shape[1], axis=1
+    )
     gate_raw, inner_raw, state_raw, step_raw = tuple(
         (jnp.dot(segment, weight, preferred_element_type=jnp.float32) for weight in weights)
     )

time: 203 us -> 210 us (1.034)
  local copies, waits for them, and re-layouts: 14.2 us -> 19.8 us
    ppermute x0 -> x3, waiting for transfers between devices: none -> 29 us  [on_device(): lax.ppermute(ring[-1], 'tp', [(dev, (dev + 1) % 4) for dev in range(4)])]
    all_gather x1 -> x0, waiting for transfers between devices: 28.4 us -> none  [on_device(): segment = lax.all_gather(tokens, 'tp', axis=1, tiled=True)]
    unnamed x33 -> x52, local copies, waits for them, and re-layouts: 1.64 us -> 7.15 us
  transfers between devices with their start and end apart: 4 -> 6, of which waited for: 3 -> 5; matrix products, arithmetic and copies ran while one was open for 6% -> 6% of each run, Pallas kernels for 0% -> 0%
where the time goes in v1:
time: 210 us
  waiting for transfers between devices  87.8 us (42%)
  matrix products  50.3 us (24%)
  blocking collectives  27.5 us (13%)
  local copies, waits for them, and re-layouts  19.8 us (9%)
  between operations  13.8 us (7%)
  other arithmetic  5.98 us (3%)
  starting transfers between devices  4.76 us (2%)
    reduce_scatter x1, waiting for transfers between devices, on_device(): lax.psum_scatter(jnp.dot(normed, out_weight, preferred_element_type=jnp.f...  33.5 us
    ppermute x3, waiting for transfers between devices, on_device(): lax.ppermute(ring[-1], 'tp', [(dev, (dev + 1) % 4) for dev in range(4)])  29 us
    all_gather x1, waiting for transfers between devices, receive(): lax.all_gather(local_state[None].astype(jnp.bfloat16), 'seq', axis=0, til...  25.2 us
    all_gather x1, blocking collectives, receive(): decay_all = lax.all_gather(decay_total[None, :], 'seq', axis=0, tiled=True)  21.9 us
    dot_general x4, matrix products, on_device(): jnp.dot(segment, weight, preferred_element_type=jnp.float32)  19.9 us
    dot_general x1, matrix products, on_device(): jnp.dot(normed, out_weight, preferred_element_type=jnp.float32)  8.78 us
    unnamed x52, local copies, waits for them, and re-layouts  7.15 us
    dot_general x2, matrix products, group_intra(): jnp.einsum('hts,shp->thp', mixing, inner_blk, preferred_element_type=jnp....  6.67 us
  transfers between devices with their start and end apart: 6, of which 5 were waited for; matrix products, arithmetic and copies ran while one was open for 6% of the time, Pallas kernels for 0%

profile of v1, /device:TPU:0, one launch (start us, length us, event | category | flops | bytes accessed | tf_op | source)
XLA Modules:
  0.0 209.9 jit_solution(1927954254855941617)
XLA Ops:
  7.0 10.4 %collective-permute-done = bf16[512,640]{1,0:T(8,128)(2,1)S(1)} collective-permute-done((bf16[512,640]{1,0:T(8,128)(2,1)}, bf16[512,640]{1,0:T(8,128)(2,1)S(1)}, u32[]{:S(2)}, u32[]{:S(2)}) %collective-permute-start) | collective-permute-done | bytes 655392 | tf_op jit(solution)/shard_map/ppermute | solution.py:87
  17.5 10.0 %collective-permute-done.1 = bf16[512,640]{1,0:T(8,128)(2,1)S(1)} collective-permute-done((bf16[512,640]{1,0:T(8,128)(2,1)S(1)}, bf16[512,640]{1,0:T(8,128)(2,1)S(1)}, u32[]{:S(2)}, u32[]{:S(2)}) %collective-permute-start.1) | collective-permute-done | bytes 655392 | tf_op jit(solution)/shard_map/ppermute | solution.py:87
  27.5 0.7 constant_dynamic-update-slice_fusion.9
  29.0 8.6 %collective-permute-done.2 = bf16[512,640]{1,0:T(8,128)(2,1)} collective-permute-done((bf16[512,640]{1,0:T(8,128)(2,1)S(1)}, bf16[512,640]{1,0:T(8,128)(2,1)}, u32[]{:S(2)}, u32[]{:S(2)}) %collective-permute-start.2) | collective-permute-done | bytes 655392 | tf_op jit(solution)/shard_map/ppermute | solution.py:87
  37.6 1.2 constant_dynamic-update-slice_fusion.7
  39.3 1.3 constant_dynamic-update-slice_fusion.3
  41.0 2.3 %copy-done.4 = bf16[512,5120]{1,0:T(8,128)(2,1)} copy-done((bf16[512,5120]{1,0:T(8,128)(2,1)}, bf16[512,5120]{1,0:T(8,128)(2,1)S(1)}, u32[]{:S(2)}) %copy-start.4) | copy-done | bytes 5242904
  43.3 1.2 negate_multiply_fusion
  46.5 7.5 %convolution_convert_fusion.2 = bf16[512,1280]{1,0:T(8,128)(2,1)S(1)} fusion(bf16[2560,1280]{1,0:T(8,128)(2,1)} %param.14, bf16[512,5120]{1,0:T(8,128)(2,1)} %copy-done.4, s32[]{:T(128)S(6)} %select_n.33), kind=kOutput, calls=%fused_computation.7 | convolution fusion | flops 3356098560 | bytes 10485764 | tf_op jit(solution)/shard_map/dot_general | solution.py:92
  54.0 1.2 fusion.44
  55.2 4.2 %collective-permute-start.3 = (bf16[3,1536]{1,0:T(4,128)(2,1)S(1)}, bf16[3,1536]{1,0:T(4,128)(2,1)S(1)}, u32[]{:S(2)}, u32[]{:S(2)}) collective-permute-start(bf16[3,1536]{1,0:T(4,128)(2,1)S(1)} %fusion.71), channel_id=1, source_target_pairs={{0,4},{4,8},{8,12},{12,16},{16,20},{20,24},{24,28},{1,5},{5,9},{9,... | collective-permute-start | bytes 27656 | tf_op jit(solution)/shard_map/ppermute | solution.py:13
  59.7 0.7 slice_bitcast_fusion.3
  61.3 2.0 multiply_convert_fusion.2
  63.3 0.9 fusion.78
  64.2 2.2 %copy.34 = bf16[256,1280]{0,1:T(8,128)(2,1)} copy(bf16[256,1280]{1,0:T(8,128)(2,1)} %get-tuple-element.12) | data formatting | bytes 1310720 | tf_op jit(solution)/shard_map/slice | solution.py:121
  66.4 1.1 copy.39
  67.5 1.9 fusion.35
  69.3 2.6 %fusion.41 = bf16[20,64,128]{2,1,0:T(8,128)(2,1)} fusion(bf16[256,20,64]{0,2,1:T(8,128)(2,1)} %bitcast.65, f32[256,20]{0,1:T(8,128)} %get-tuple-element.17, f32[20,64,128]{2,1,0:T(8,128)S(1)} %fusion.35, f32[20]{0:T(128)S(1)} %get-tuple-element.23, f32[20]{0:T(128)S(1)} %exp.52, bf16[512,1536]{1,0:T(8,128)(2,1)S(1)} %multiply_convert_fusion.2), kind=kOutput, calls=%fused_computation.56 | convolution fusion | flops 504627200 | bytes 1725440 | tf_op jit(solution)/shard_map/thp,tn->hpn/dot_general | solution.py:21
  74.1 21.9 %all-gather.1 = f32[8,1,20]{2,1,0:T(1,128)S(1)} all-gather(f32[1,1,20]{2,1,0:T(1,128)S(1)} %bitcast.82), channel_id=1, replica_groups=mesh['seq'=8,'tp'=4] {'seq'}, dimensions={0}, use_global_device_ids=true | all-gather | bytes 720 | tf_op jit(solution)/shard_map/all_gather | solution.py:57
  96.6 3.9 %fusion.27 = f32[256,20,64]{0,2,1:T(8,128)} fusion(bf16[256,20,64]{0,2,1:T(8,128)(2,1)} %bitcast.68, f32[20,256]{1,0:T(8,128)} %get-tuple-element.14, f32[20,256]{1,0:T(8,128)} %bitcast.76, f32[256,256]{1,0:T(8,128)S(1)} %fusion.65, pred[256,256]{1,0:T(8,128)(4,1)} %iota_compare_fusion), kind=kOutput, calls=%fused_computation.42 | convolution fusion | flops 174325760 | bytes 2334720 | tf_op jit(solution)/shard_map/hts,shp->thp/dot_general | solution.py:34
  100.5 2.8 %fusion.26 = f32[256,20,64]{0,2,1:T(8,128)} fusion(bf16[256,20,64]{0,2,1:T(8,128)(2,1)S(1)} %bitcast.66, f32[20,256]{1,0:T(8,128)S(1)} %copy-done.12, f32[20,256]{1,0:T(8,128)S(1)} %bitcast.73, f32[256,256]{1,0:T(8,128)S(1)} %fusion.60, pred[256,256]{1,0:T(8,128)(4,1)S(1)} %copy-done.11), kind=kOutput, calls=%fused_computation.41 | convolution fusion | flops 174325760 | bytes 2334720 | tf_op jit(solution)/shard_map/hts,shp->thp/dot_general | solution.py:34
  103.3 25.2 %all-gather.4.cloned.1.call-done = bf16[160,64,128]{2,1,0:T(8,128)(2,1)} async-done(((bf16[20,64,128]{2,1,0:T(8,128)(2,1)}), bf16[160,64,128]{2,1,0:T(8,128)(2,1)}) %all-gather.4.cloned.1.call-update) | async-done | bytes 2621456 | tf_op jit(solution)/shard_map/all_gather | solution.py:62
  128.5 5.0 %fusion.6 = f32[20,1,64,128]{3,1,2,0:T(1,128)S(1)} fusion(f32[8,20,1,1]{0,2,3,1:T(1,128)S(1)} %copy.43, bf16[8,20,64,128]{3,2,1,0:T(8,128)(2,1)} %bitcast.64), kind=kOutput, calls=%fused_computation.15 | convolution fusion | flops 15728640 | bytes 3277440 | tf_op jit(solution)/shard_map/kh,khpn->hpn/dot_general | solution.py:50
  133.5 0.8 copy-done.1
  134.3 1.8 fusion.28
  136.1 2.9 %copy.40 = f32[256,1280]{1,0:T(8,128)} copy(f32[256,1280]{0,1:T(8,128)} %bitcast.62) | data formatting | bytes 2621440 | tf_op jit(solution)/shard_map/concatenate | solution.py:145
  139.0 3.3 %fusion.29 = f32[256,20,64]{0,2,1:T(8,128)} fusion(f32[256,20,64]{0,2,1:T(8,128)} %fusion.26, f32[256,20]{0,1:T(8,128)} %get-tuple-element.20, f32[20,64,128]{2,1,0:T(8,128)S(1)} %fusion.35, f32[20,64,128]{2,1,0:T(8,128)} %bitcast.61, f32[20]{0:T(128)S(1)} %copy-done.16, bf16[512,1536]{1,0:T(8,128)(2,1)S(1)} %multiply_convert_fusion.2), kind=kOutput, calls=%fused_computation.46 | convolution fusion | flops 504299520 | bytes 4018688 | tf_op jit(solution)/shard_map/tn,hpn->thp/dot_general | solution.py:38
  142.3 2.8 %copy.41 = f32[256,1280]{1,0:T(8,128)} copy(f32[256,1280]{0,1:T(8,128)} %bitcast.63) | data formatting | bytes 2621440 | tf_op jit(solution)/shard_map/concatenate | solution.py:145
  145.1 10.1 %multiply_reduce_fusion = (f32[512]{0:T(512)S(1)}, f32[512,1280]{1,0:T(8,128)}) fusion(bf16[2560,1280]{1,0:T(8,128)(2,1)} %param.13, bf16[512,5120]{1,0:T(8,128)(2,1)} %copy-done.4, s32[]{:T(128)S(6)} %select_n.33, bf16[512,1536]{1,0:T(8,128)(2,1)S(1)} %multiply_convert_fusion.2, f32[1280]{0:T(1024)S(1)} %copy-done.13, f32[256,1280]{1,0:T(8,128)} %copy.41, ...), kind=kOutput, calls=%fused_computation.18 | convolution fusion | flops 3363962368 | bytes 15735812 | tf_op jit(solution)/shard_map/dot_general | solution.py:92
  155.2 5.6 %psum.7 = f32[512]{0:T(512)S(1)} all-reduce(f32[512]{0:T(512)S(1)} %get-tuple-element.26), channel_id=1, replica_groups=mesh['seq'=8,'tp'=4] {'tp'}, use_global_device_ids=true, to_apply=%region_6.7 | all-reduce | flops 512 | bytes 4096 | tf_op jit(solution)/shard_map/psum | solution.py:149
  160.8 8.8 %convolution_convert_fusion = bf16[512,2560]{1,0:T(8,128)(2,1)} fusion(bf16[1280,2560]{1,0:T(8,128)(2,1)} %param.23, f32[512,1280]{1,0:T(8,128)} %get-tuple-element.27, f32[1280]{0:T(1024)S(1)} %copy-done.17, f32[512]{0:T(512)S(1)} %add_rsqrt_fusion), kind=kOutput, calls=%fused_computation.2 | convolution fusion | flops 3358720000 | bytes 11803648 | tf_op jit(solution)/shard_map/dot_general | solution.py:155
  169.6 33.5 %reduce-scatter.2.cloned.1.call-done = bf16[128,2560]{1,0:T(8,128)(2,1)} async-done(((bf16[512,2560]{1,0:T(8,128)(2,1)}), bf16[128,2560]{1,0:T(8,128)(2,1)}) %reduce-scatter.2.cloned.1.call-update) | async-done | bytes 655376 | tf_op jit(solution)/shard_map/reduce_scatter | solution.py:154
  (93 shorter events, 7.9 us)
Async XLA Ops:
  6.5 47.5 %copy-start = (bf16[2560,256]{1,0:T(8,128)(2,1)S(1)}, bf16[2560,256]{1,0:T(8,128)(2,1)}, u32[]{:S(2)}) copy-start(bf16[2560,256]{1,0:T(8,128)(2,1)} %param.15) | copy-start | bytes 3932164
  6.5 32.5 %copy-start.2 = (bf16[512,640]{1,0:T(8,128)(2,1)S(1)}, bf16[512,640]{1,0:T(8,128)(2,1)}, u32[]{:S(2)}) copy-start(bf16[512,640]{1,0:T(8,128)(2,1)} %param.12) | copy-start | bytes 1966084
  6.5 121.9 %all-gather.4.cloned.1.call-start = ((), (), s32[]{:S(2)}) async-start(), calls=%async_computation.2 | async-start | bytes 2949120 | tf_op jit(solution)/shard_map/all_gather | solution.py:62
  6.5 10.9 %collective-permute-start = (bf16[512,640]{1,0:T(8,128)(2,1)}, bf16[512,640]{1,0:T(8,128)(2,1)S(1)}, u32[]{:S(2)}, u32[]{:S(2)}) collective-permute-start(bf16[512,640]{1,0:T(8,128)(2,1)} %param.12), channel_id=1, source_target_pairs={{0,1},{1,2},{2,3},{3,0},{4,5},{5,6},{6,7},{7,4},{8,9},{9,10},{10,1... | collective-permute-start | bytes 1966088 | tf_op jit(solution)/shard_map/ppermute | solution.py:87
  17.5 10.0 %collective-permute-start.1 = (bf16[512,640]{1,0:T(8,128)(2,1)S(1)}, bf16[512,640]{1,0:T(8,128)(2,1)S(1)}, u32[]{:S(2)}, u32[]{:S(2)}) collective-permute-start(bf16[512,640]{1,0:T(8,128)(2,1)S(1)} %collective-permute-done), channel_id=1, source_target_pairs={{0,1},{1,2},{2,3},{3,0},{4,5},{5,6},{6,7},{7,4},{8,9},{9,10},{10,1... | collective-permute-start | bytes 1966088 | tf_op jit(solution)/shard_map/ppermute | solution.py:87
  27.5 10.1 %collective-permute-start.2 = (bf16[512,640]{1,0:T(8,128)(2,1)S(1)}, bf16[512,640]{1,0:T(8,128)(2,1)}, u32[]{:S(2)}, u32[]{:S(2)}) collective-permute-start(bf16[512,640]{1,0:T(8,128)(2,1)S(1)} %collective-permute-done.1), channel_id=1, source_target_pairs={{0,1},{1,2},{2,3},{3,0},{4,5},{5,6},{6,7},{7,4},{8,9},{9,10},{10,1... | collective-permute-start | bytes 1966088 | tf_op jit(solution)/shard_map/ppermute | solution.py:87
  39.2 4.1 %copy-start.9 = (bf16[2560,20]{0,1:T(8,128)(2,1)S(1)}, bf16[2560,20]{0,1:T(8,128)(2,1)}, u32[]{:S(2)}) copy-start(bf16[2560,20]{0,1:T(8,128)(2,1)} %param.16) | copy-start | bytes 307204
  39.2 4.1 %copy-start.14 = (f32[20]{0:T(128)S(1)}, f32[20]{0:T(128)}, u32[]{:S(2)}) copy-start(f32[20]{0:T(128)} %param.20) | copy-start | bytes 244
  39.3 4.1 %copy-start.15 = (f32[20]{0:T(128)S(1)}, f32[20]{0:T(128)}, u32[]{:S(2)}) copy-start(f32[20]{0:T(128)} %param.19) | copy-start | bytes 244
  41.0 2.3 %copy-start.4 = (bf16[512,5120]{1,0:T(8,128)(2,1)}, bf16[512,5120]{1,0:T(8,128)(2,1)S(1)}, u32[]{:S(2)}) copy-start(bf16[512,5120]{1,0:T(8,128)(2,1)S(1)} %constant_dynamic-update-slice_fusion) | copy-start | bytes 15728644
  45.5 8.6 %slice-start = ((s8[5242880]{0:T(1024)(128)(4,1)}), s8[1048576]{0:T(1024)(128)(4,1)S(1)}, s32[]{:S(2)}) async-start(s8[5242880]{0:T(1024)(128)(4,1)} %bitcast.69), calls=%async_computation.3 | async-start | bytes 2097152
  45.5 14.2 %copy-start.6 = (f32[3,8,2,128]{3,1,2,0:T(8,128)}, f32[3,8,2,128]{3,1,2,0:T(8,128)S(1)}, u32[]{:S(2)}) copy-start(f32[3,8,2,128]{3,1,2,0:T(8,128)S(1)} %copy.47) | copy-start | bytes 73732
  46.5 13.2 %copy-start.8 = (f32[3,8,2,128]{3,1,2,0:T(8,128)}, f32[3,8,2,128]{3,1,2,0:T(8,128)S(1)}, u32[]{:S(2)}) copy-start(f32[3,8,2,128]{3,1,2,0:T(8,128)S(1)} %copy.46) | copy-start | bytes 73732
  46.5 7.6 %slice-start.1 = ((s8[5242880]{0:T(1024)(128)(4,1)}), s8[4194304]{0:T(1024)(128)(4,1)S(1)}, s32[]{:S(2)}) async-start(s8[5242880]{0:T(1024)(128)(4,1)} %bitcast.69), calls=%async_computation.4 | async-start | bytes 8388608
  55.2 5.7 %collective-permute-start.3 = (bf16[3,1536]{1,0:T(4,128)(2,1)S(1)}, bf16[3,1536]{1,0:T(4,128)(2,1)S(1)}, u32[]{:S(2)}, u32[]{:S(2)}) collective-permute-start(bf16[3,1536]{1,0:T(4,128)(2,1)S(1)} %fusion.71), channel_id=1, source_target_pairs={{0,4},{4,8},{8,12},{12,16},{16,20},{20,24},{24,28},{1,5},{5,9},{9,... | collective-permute-start | bytes 27656 | tf_op jit(solution)/shard_map/ppermute | solution.py:13
  72.0 131.1 %reduce-scatter.2.cloned.1.call-start = ((), (), s32[]{:S(2)}) async-start(), calls=%async_computation.1 | async-start | bytes 3276800 | tf_op jit(solution)/shard_map/reduce_scatter | solution.py:154
  96.5 4.0 %copy-start.3 = (bf16[256,1280]{0,1:T(8,128)(2,1)S(1)}, bf16[256,1280]{0,1:T(8,128)(2,1)}, u32[]{:S(2)}) copy-start(bf16[256,1280]{0,1:T(8,128)(2,1)} %copy.39) | copy-start | bytes 1966084
  96.5 4.0 %copy-start.7 = (f32[3,8,2,128]{3,1,2,0:T(8,128)S(1)}, f32[3,8,2,128]{3,1,2,0:T(8,128)}, u32[]{:S(2)}) copy-start(f32[3,8,2,128]{3,1,2,0:T(8,128)} %copy-done.6) | copy-start | bytes 73732
  96.6 3.9 %copy-start.11 = (pred[256,256]{1,0:T(8,128)(4,1)S(1)}, pred[256,256]{1,0:T(8,128)(4,1)}, u32[]{:S(2)}) copy-start(pred[256,256]{1,0:T(8,128)(4,1)} %iota_compare_fusion) | copy-start | bytes 196612
  96.6 3.9 %copy-start.12 = (f32[20,256]{1,0:T(8,128)S(1)}, f32[20,256]{1,0:T(8,128)}, u32[]{:S(2)}) copy-start(f32[20,256]{1,0:T(8,128)} %get-tuple-element.16) | copy-start | bytes 61444
  128.5 5.8 %copy-start.5 = (f32[256,20,64]{0,2,1:T(8,128)S(1)}, f32[256,20,64]{0,2,1:T(8,128)}, u32[]{:S(2)}) copy-start(f32[256,20,64]{0,2,1:T(8,128)} %fusion.27) | copy-start | bytes 3932164
  128.5 5.8 %copy-start.10 = (f32[256,20]{0,1:T(8,128)S(1)}, f32[256,20]{0,1:T(8,128)}, u32[]{:S(2)}) copy-start(f32[256,20]{0,1:T(8,128)} %get-tuple-element.21) | copy-start | bytes 61444
  133.4 0.8 copy-start.1
  134.3 4.7 %copy-start.16 = (f32[20]{0:T(128)S(1)}, f32[20]{0:T(128)}, u32[]{:S(2)}) copy-start(f32[20]{0:T(128)} %get-tuple-element.22) | copy-start | bytes 244
  139.0 6.1 %copy-start.13 = (f32[1280]{0:T(1024)S(1)}, f32[1280]{0:T(1024)}, u32[]{:S(2)}) copy-start(f32[1280]{0:T(1024)} %mul.230) | copy-start | bytes 15364
  145.1 15.7 %copy-start.17 = (f32[1280]{0:T(1024)S(1)}, f32[1280]{0:T(1024)}, u32[]{:S(2)}) copy-start(f32[1280]{0:T(1024)} %param.22) | copy-start | bytes 15364
Sparse Core Ops, SparseCore 0:
  72.1 56.3 all-gather.3
  169.7 33.3 reduce-scatter.1
